TPU v7x, 32 devices: a whole 2x2x4 slice. The times are simulated.
32 devices in a mesh: shard: 8 (over y, x, core), width: 4 (over z).
Axes of the slice: x: 2, y: 2, z: 4, core: 2. Of those that a mesh axis runs over, the one named last changes fastest.
Arguments:
- w_up: bfloat16 [12288, 49152], P('shard', 'width'), may hold values from -0.078125 to 0.078125
- low_up: bfloat16 [12288, 64], P('shard'), may hold values from -0.0546875 to 0.0546875
- high_up: bfloat16 [64, 49152], P(None, 'width'), may hold values from -0.75 to 0.75
- norm_train: float32 [12288], P(('shard', 'width')), may hold values from 0.25 to 1.75
- norm_step: float32 [12288], P(('shard', 'width')), may hold values from -0.3 to 0.3
Outputs:
- serve_up: bfloat16 [12288, 49152], P(None, ('width', 'shard'))
- scale_up: float32 [49152], P(('width', 'shard'))
- serve_norm: bfloat16 [12288], replicated
All inputs are finite; a program needn't handle non-finite values. Where the computation divides by a largest or mean magnitude, that divisor is 1e-20 or more.
Results may differ from a plain program's by a relative error of at most 0.001.
Values may be sent and summed in bfloat16 or wider, within the bound.
A program may use at most 256 MiB of HBM per device.

v0:
```python
import jax
import jax.numpy as jnp
from jax import lax
from jax.sharding import PartitionSpec as P

D_MODEL = 12288


mix_rate = 0.5


def per_device(w_up, low_up, high_up, norm_train, norm_step):
    fresh_up = w_up.astype(jnp.float32) + mix_rate * jnp.dot(
        low_up, high_up, preferred_element_type=jnp.float32
    )
    total_up = lax.psum(jnp.sum(jnp.abs(fresh_up), axis=0), "shard")
    scale_up = total_up / D_MODEL
    narrow_up = (fresh_up / scale_up).astype(jnp.bfloat16)
    serve_up = lax.all_to_all(narrow_up, "shard", split_axis=1, concat_axis=0, tiled=True)
    place = lax.axis_index("shard")
    scale_up = lax.dynamic_slice_in_dim(scale_up, place * serve_up.shape[1], serve_up.shape[1])
    serve_norm = lax.all_gather(
        (norm_train + norm_step).astype(jnp.bfloat16), ("shard", "width"), axis=0, tiled=True
    )
    return (serve_up, scale_up, serve_norm)


def solution(mesh):
    placed = (
        P("shard", "width"),
        P("shard", None),
        P(None, "width"),
        P(("shard", "width")),
        P(("shard", "width")),
    )
    return jax.shard_map(
        per_device,
        mesh=mesh,
        in_specs=placed,
        out_specs=(P(None, ("width", "shard")), P(("width", "shard")), P()),
        check_vma=False,
    )
```

profile of v0, /device:TPU:0, one launch (start us, length us, event | category | flops | bytes accessed | tf_op | source)
XLA Modules:
  0.0 570.9 jit_solution(10614602594228669875)
XLA Ops:
  0.6 0.0 copy-start
  0.6 1.4 copy-done
  2.0 38.1 %abs_reduce_fusion = (f32[12288]{0:T(1024)S(1)}, f32[1536,12288]{1,0:T(8,128)}) fusion(bf16[1536,64]{0,1:T(8,128)(2,1)} %param.6, bf16[64,12288]{1,0:T(8,128)(2,1)S(1)} %copy-done, bf16[1536,12288]{1,0:T(8,128)(2,1)} %param.5), kind=kOutput, calls=%fused_computation.1 | convolution fusion | flops 2510278656 | bytes 115064832 | tf_op jit(solution)/shard_map/dot_general | solution.py:13
  40.1 26.0 %psum.7 = f32[12288]{0:T(1024)S(1)} all-reduce(f32[12288]{0:T(1024)S(1)} %get-tuple-element.3), channel_id=1, replica_groups=mesh['shard'=8,'width'=4] {'shard'}, use_global_device_ids=true, to_apply=%region_1.0 | all-reduce | flops 12288 | bytes 98304 | tf_op jit(solution)/shard_map/psum | solution.py:16
  66.2 36.5 %divide_convert_fusion = bf16[1536,12288]{1,0:T(8,128)(2,1)} fusion(f32[1536,12288]{1,0:T(8,128)} %get-tuple-element.4, f32[12288]{0:T(1024)S(1)} %broadcast_multiply_fusion), kind=kLoop, calls=%fused_computation | loop fusion | flops 37748736 | bytes 113295360 | tf_op jit(solution)/shard_map/convert_element_type | solution.py:18
  102.7 26.0 %copy.13 = bf16[192,8,8,1536]{3,2,0,1:T(8,128)(2,1)} copy(bf16[192,8,8,1536]{3,2,1,0:T(8,128)(2,1)} %bitcast.10) | data formatting | bytes 75497472 | tf_op jit(solution)/shard_map/all_to_all | solution.py:19
  128.6 0.0 copy-start.2
  128.6 0.0 copy-start.3
  128.7 7.6 %all-to-all-start = ((bf16[1536,8,1536]{2,0,1:T(8,128)(2,1)}), bf16[1536,8,1536]{2,0,1:T(8,128)(2,1)}, u32[]{:S(2)}, u32[]{:S(2)}) async-start(bf16[1536,8,1536]{2,0,1:T(8,128)(2,1)} %bitcast.9), calls=%async_computation | async-start | bytes 75497472 | tf_op jit(solution)/shard_map/all_to_all | solution.py:19
  136.3 0.7 dynamic_slice.3
  136.9 0.0 copy-done.2
  136.9 0.0 copy-done.3
  137.0 71.3 %all-gather = bf16[32,1,384]{2,1,0:T(2,128)(2,1)S(1)} all-gather(bf16[1,1,384]{2,1,0:T(2,128)(2,1)S(1)} %reshape.10), channel_id=1, replica_groups=mesh['shard'=8,'width'=4] {'shard','width'}, dimensions={0}, use_global_device_ids=true | all-gather | bytes 25344 | tf_op jit(solution)/shard_map/all_gather | solution.py:22
  208.3 0.1 reduce
  208.4 0.6 reshape.11
  209.0 336.1 %all-to-all-done = bf16[1536,8,1536]{2,0,1:T(8,128)(2,1)} async-done(((bf16[1536,8,1536]{2,0,1:T(8,128)(2,1)}), bf16[1536,8,1536]{2,0,1:T(8,128)(2,1)}, u32[]{:S(2)}, u32[]{:S(2)}) %all-to-all-start) | async-done | bytes 37748768 | tf_op jit(solution)/shard_map/all_to_all | solution.py:19
  545.1 0.0 copy-start.1
  545.1 25.7 %copy.15 = bf16[12288,1536]{1,0:T(8,128)(2,1)} copy(bf16[12288,1536]{1,0:T(8,128)(2,1)} %bitcast.1) | data formatting | bytes 75497472
  570.9 0.0 copy-done.1
  (3 shorter events, 0.0 us)
Async XLA Ops:
  0.6 1.4 copy-start
  128.6 8.3 %copy-start.2 = (f32[384]{0:T(512)S(1)}, f32[384]{0:T(512)}, u32[]{:S(2)}) copy-start(f32[384]{0:T(512)} %param.8) | copy-start | bytes 4612
  128.6 8.3 %copy-start.3 = (f32[384]{0:T(512)S(1)}, f32[384]{0:T(512)}, u32[]{:S(2)}) copy-start(f32[384]{0:T(512)} %param.9) | copy-start | bytes 4612
  128.7 416.5 %all-to-all-start = ((bf16[1536,8,1536]{2,0,1:T(8,128)(2,1)}), bf16[1536,8,1536]{2,0,1:T(8,128)(2,1)}, u32[]{:S(2)}, u32[]{:S(2)}) async-start(bf16[1536,8,1536]{2,0,1:T(8,128)(2,1)} %bitcast.9), calls=%async_computation | async-start | bytes 75497472 | tf_op jit(solution)/shard_map/all_to_all | solution.py:19
  545.1 25.8 %copy-start.1 = (bf16[64,12288]{1,0:T(8,128)(2,1)S(1)}, bf16[64,12288]{1,0:T(8,128)(2,1)}, u32[]{:S(2)}) copy-start(bf16[64,12288]{1,0:T(8,128)(2,1)} %param.7) | copy-start | bytes 4718596
where the time goes:
time: 571 us
  waiting for transfers between devices  336 us (59%)
  blocking collectives  97.4 us (17%)
  local copies, waits for them, and re-layouts  54.5 us (10%)
  matrix products  38.1 us (7%)
  other arithmetic  36.6 us (6%)
  starting transfers between devices  7.59 us (1%)
    all_to_all x1, waiting for transfers between devices, per_device(): lax.all_to_all(narrow_up, 'shard', split_axis=1, concat_axis=0, tiled=True)  336 us
    all_gather x1, blocking collectives, per_device(): lax.all_gather((norm_train + norm_step).astype(jnp.bfloat16), ('shard', '...  71.3 us
    dot_general x1, matrix products, per_device(): jnp.dot(low_up, high_up, preferred_element_type=jnp.float32)  38.1 us
    convert_element_type x1, other arithmetic, per_device(): narrow_up = (fresh_up / scale_up).astype(jnp.bfloat16)  36.5 us
    unnamed x11, local copies, waits for them, and re-layouts  27.8 us
    psum x1, blocking collectives, per_device(): total_up = lax.psum(jnp.sum(jnp.abs(fresh_up), axis=0), 'shard')  26 us
    all_to_all x1, local copies, waits for them, and re-layouts, per_device(): lax.all_to_all(narrow_up, 'shard', split_axis=1, concat_axis=0, tiled=True)  26 us
  transfers between devices with their start and end apart: 1, of which 1 were waited for; matrix products, arithmetic and copies ran while one was open for 0% of the time, Pallas kernels for 0%

commit v1 on v0

v1 whole, which is shorter than its diff:
```python
import functools

import jax
import jax.numpy as jnp
from jax import lax
from jax.experimental import pallas as pl
from jax.experimental.pallas import tpu as pltpu
from jax.sharding import PartitionSpec as P

MESH = pl.DeviceIdType.MESH

mix_rate = 0.5


def tile_of(extent, most):
    for size in range(most, 0, -128):
        if extent % size == 0:
            return size
    return extent


def contract_first(a, b):
    return lax.dot_general(a, b, (((0,), (0,)), ((), ())), preferred_element_type=jnp.float32)


def exchange_kernel(
    n, depth, w_ref, low_ref, high_ref, small_ref,
    g_ref, all_ref, mine_ref, parts_ref,
    send_sem, recv_sem, small_send, small_recv, far_send, far_recv, part_send, part_recv, own_sem,
):
    me = lax.axis_index("shard")
    z = lax.axis_index("width")
    rows = w_ref.shape[0]
    rank = low_ref.shape[0]
    cols = g_ref.shape[1]
    order = sorted(range(1, n), key=lambda k: (bin(k >> 1).count("1"), k))

    def columns(p):
        return pl.ds(pl.multiple_of(p * cols, cols), cols)

    def rows_of(p):
        return pl.ds(pl.multiple_of(p * rows, rows), rows)

    def small_copy(k):
        return pltpu.make_async_remote_copy(
            src_ref=small_ref, dst_ref=all_ref.at[me, z],
            send_sem=small_send.at[k], recv_sem=small_recv.at[k],
            device_id={"shard": me ^ k}, device_id_type=MESH,
        )

    def big_copy(k):
        return pltpu.make_async_remote_copy(
            src_ref=w_ref.at[:, columns(me ^ k)], dst_ref=g_ref.at[rows_of(me), :],
            send_sem=send_sem.at[k], recv_sem=recv_sem.at[k],
            device_id={"shard": me ^ k}, device_id_type=MESH,
        )

    def part_copy(k):
        return pltpu.make_async_remote_copy(
            src_ref=mine_ref.at[:, columns(me ^ k)], dst_ref=parts_ref.at[me],
            send_sem=part_send.at[k], recv_sem=part_recv.at[k],
            device_id={"shard": me ^ k}, device_id_type=MESH,
        )

    def far_copy(k):
        return pltpu.make_async_remote_copy(
            src_ref=all_ref.at[:, z], dst_ref=all_ref.at[:, z],
            send_sem=far_send.at[k], recv_sem=far_recv.at[k],
            device_id={"width": z ^ k}, device_id_type=MESH,
        )

    own_small = pltpu.make_async_copy(small_ref, all_ref.at[me, z], own_sem.at[0])
    own_small.start()
    for k in order:
        small_copy(k).start()
    for k in order:
        big_copy(k).start()

    own_small.wait()
    for k in order:
        small_copy(k).wait()
    for k in range(1, depth):
        far_copy(k).start()

    tile = tile_of(w_ref.shape[1], 512)
    step = tile_of(rows, 256)

    def add_up(w_tile, high_tile, sum_tile):
        total = jnp.zeros((8, tile), jnp.float32)
        for r in range(0, rows, step):
            fresh = w_tile[r:r + step, :].astype(jnp.float32) + mix_rate * contract_first(
                low_ref[:, r:r + step], high_tile[...]
            )
            total = total + jnp.sum(jnp.abs(fresh).reshape(step // 8, 8, tile), axis=0)
        sum_tile[...] = jnp.sum(total, axis=0, keepdims=True)

    pltpu.emit_pipeline(
        add_up,
        grid=(w_ref.shape[1] // tile,),
        in_specs=[
            pl.BlockSpec((rows, tile), lambda j: (0, j)),
            pl.BlockSpec((rank, tile), lambda j: (0, j)),
        ],
        out_specs=[pl.BlockSpec((1, tile), lambda j: (0, j))],
    )(w_ref, high_ref, mine_ref)

    own_part = pltpu.make_async_copy(mine_ref.at[:, columns(me)], parts_ref.at[me], own_sem.at[1])
    own_part.start()
    for k in order:
        part_copy(k).start()

    band = tile_of(rows, 384)

    def take_over(source, target):
        target[...] = source[...]

    pltpu.emit_pipeline(
        take_over,
        grid=(rows // band,),
        in_specs=[pl.BlockSpec((band, cols), lambda i: (i, me))],
        out_specs=[pl.BlockSpec((band, cols), lambda i: (me * (rows // band) + i, 0))],
    )(w_ref, g_ref)

    own_part.wait()
    for k in range(1, depth):
        far_copy(k).wait()
    for k in order:
        part_copy(k).wait()
    for k in order:
        big_copy(k).wait()


def finish_kernel(inner, w_ref, small_ref, high_ref, parts_ref, out_ref, scale_ref):
    rank = high_ref.shape[0]
    height = w_ref.shape[0]
    scale = jnp.sum(parts_ref[...], axis=0) / inner
    scale_ref[...] = scale
    inverse = 1.0 / scale
    step = tile_of(height, 128)
    for r in range(0, height, step):
        fresh = w_ref[r:r + step, :].astype(jnp.float32) + contract_first(
            small_ref[:rank, r:r + step], high_ref[...]
        )
        out_ref[r:r + step, :] = (fresh * inverse).astype(jnp.bfloat16)


def solution(mesh):
    n, depth = mesh.shape["shard"], mesh.shape["width"]

    def per_device(w_up, low_up, high_up, norm_train, norm_step):
        rows, wide = w_up.shape
        rank = low_up.shape[1]
        cols = wide // n
        part = rows // depth
        me = lax.axis_index("shard")
        z = lax.axis_index("width")
        low = low_up.T
        gain = (norm_train + norm_step).astype(jnp.bfloat16).reshape(1, part)
        small = jnp.concatenate(
            [
                lax.dynamic_slice_in_dim(low, z * part, part, axis=1) * jnp.bfloat16(mix_rate),
                jnp.broadcast_to(gain, (16, part)),
            ],
            axis=0,
        )
        high_own = lax.dynamic_slice_in_dim(high_up, me * cols, cols, axis=1)
        any_spec = pl.BlockSpec(memory_space=pl.ANY)
        dma = pltpu.SemaphoreType.DMA
        gathered, everyone, _, parts = pl.pallas_call(
            functools.partial(exchange_kernel, n, depth),
            out_shape=(
                jax.ShapeDtypeStruct((n * rows, cols), jnp.bfloat16),
                jax.ShapeDtypeStruct((n, depth) + small.shape, jnp.bfloat16),
                jax.ShapeDtypeStruct((1, wide), jnp.float32),
                jax.ShapeDtypeStruct((n, 1, cols), jnp.float32),
            ),
            in_specs=[any_spec, pl.BlockSpec(memory_space=pltpu.VMEM), any_spec, any_spec],
            out_specs=(any_spec,) * 4,
            scratch_shapes=[
                dma((n,)), dma((n,)), dma((n,)), dma((n,)), dma((depth,)), dma((depth,)),
                dma((n,)), dma((n,)), dma((2,)),
            ],
            compiler_params=pltpu.CompilerParams(has_side_effects=True),
            name="exchange",
        )(w_up, low, high_up, small)
        serve_up, scale_up = pl.pallas_call(
            functools.partial(finish_kernel, n * rows),
            grid=(n * depth,),
            out_shape=(
                jax.ShapeDtypeStruct((n * rows, cols), jnp.bfloat16),
                jax.ShapeDtypeStruct((1, cols), jnp.float32),
            ),
            in_specs=[
                pl.BlockSpec((part, cols), lambda i: (i, 0)),
                pl.BlockSpec((None, None) + small.shape, lambda i: (i // depth, i % depth, 0, 0)),
                pl.BlockSpec((rank, cols), lambda i: (0, 0)),
                pl.BlockSpec((n, 1, cols), lambda i: (0, 0, 0)),
            ],
            out_specs=(
                pl.BlockSpec((part, cols), lambda i: (i, 0)),
                pl.BlockSpec((1, cols), lambda i: (0, 0)),
            ),
            compiler_params=pltpu.CompilerParams(dimension_semantics=("arbitrary",)),
            name="finish",
        )(gathered, everyone, high_own, parts)
        serve_norm = everyone[:, :, rank, :].reshape(n * rows)
        return serve_up, scale_up.reshape(cols), serve_norm

    placed = (
        P("shard", "width"),
        P("shard", None),
        P(None, "width"),
        P(("shard", "width")),
        P(("shard", "width")),
    )
    return jax.shard_map(
        per_device,
        mesh=mesh,
        in_specs=placed,
        out_specs=(P(None, ("width", "shard")), P(("width", "shard")), P()),
        check_vma=False,
    )
```

time: 571 us -> 475 us (0.83)
  Pallas kernels: 0 us -> 466 us
  waiting for transfers between devices: 336 us -> 0 us
  blocking collectives: 97.4 us -> 0 us
  local copies, waits for them, and re-layouts: 54.5 us -> 3.3 us
  matrix products: 38.1 us -> 0 us
  other arithmetic: 36.6 us -> 3.45 us
  starting transfers between devices: 7.59 us -> 0 us
    pallas_call x0 -> x2, Pallas kernels: none -> 466 us  [the longest x1 423 us: per_device(): pl.pallas_call(functools.partial(exchange_kernel, n, depth), out_shape=(j...]
    all_to_all x1 -> x0, waiting for transfers between devices: 336 us -> none  [per_device(): lax.all_to_all(narrow_up, 'shard', split_axis=1, concat_axis=0, tiled=True)]
    all_gather x1 -> x0, blocking collectives: 71.3 us -> none  [per_device(): lax.all_gather((norm_train + norm_step).astype(jnp.bfloat16), ('shard', '...]
    dot_general x1 -> x0, matrix products: 38.1 us -> none  [per_device(): jnp.dot(low_up, high_up, preferred_element_type=jnp.float32)]
    convert_element_type x2 -> x1, other arithmetic: 36.5 us -> 0.7 us  [per_device(): gain = (norm_train + norm_step).astype(jnp.bfloat16).reshape(1, part)]
    unnamed x11 -> x0, local copies, waits for them, and re-layouts: 27.8 us -> none
    psum x1 -> x0, blocking collectives: 26 us -> none  [per_device(): total_up = lax.psum(jnp.sum(jnp.abs(fresh_up), axis=0), 'shard')]
    all_to_all x1 -> x0, local copies, waits for them, and re-layouts: 26 us -> none  [per_device(): lax.all_to_all(narrow_up, 'shard', split_axis=1, concat_axis=0, tiled=True)]
  transfers between devices with their start and end apart: 1 -> 0, of which waited for: 1 -> 0; matrix products, arithmetic and copies ran while one was open for 0% -> 0% of each run, Pallas kernels for 0% -> 0%
where the time goes in v1:
time: 475 us; the launch traced here: 473 us
  Pallas kernels  466 us (98%)
    pallas_call x1, Pallas kernels, per_device(): pl.pallas_call(functools.partial(exchange_kernel, n, depth), out_shape=(j...  423 us
    pallas_call x1, Pallas kernels, per_device(): pl.pallas_call(functools.partial(finish_kernel, n * rows), grid=(n * dept...  43 us

profile of v1, /device:TPU:0, one launch (start us, length us, event | category | flops | bytes accessed | tf_op | source)
XLA Modules:
  0.0 473.2 jit_solution(2752227816964252969)
XLA Ops:
  0.6 0.7 add_convert_fusion
  1.3 0.8 multiply_bitcast_fusion
  2.2 0.6 pad_maximum_fusion.small_ref
  2.8 1.6 constant_dynamic-slice_fusion.high_ref
  4.4 422.9 %exchange.1 = (bf16[12288,1536]{1,0:T(8,128)(2,1)}, bf16[8,4,80,384]{3,2,1,0:T(8,128)(2,1)}, f32[1,12288]{1,0:T(1,128)}, f32[8,1,1536]{2,1,0:T(1,128)}) custom-call(bf16[1536,12288]{1,0:T(8,128)(2,1)} %w_ref.1, bf16[64,1536]{1,0:T(8,128)(2,1)} %bitcast.3, bf16[64,12288]{1,0:T(8,128)(2,1)} %high_ref.1, bf16[80,384]{1,0:T(8,128)(2,1)} %pad_maximum_fusion.small_ref), custom_call_target="tpu_custom_call" | custom-call | tf_op jit(solution)/shard_map/exchange/pallas_call | solution.py:169
  427.3 43.0 %finish.1 = (bf16[12288,1536]{1,0:T(8,128)(2,1)}, f32[1,1536]{1,0:T(1,128)}) custom-call(bf16[12288,1536]{1,0:T(8,128)(2,1)} %get-tuple-element.8.w_ref, bf16[8,4,80,384]{3,2,1,0:T(8,128)(2,1)} %get-tuple-element.9.small_ref, bf16[64,1536]{1,0:T(8,128)(2,1)} %constant_dynamic-slice_fusion.high_ref, f32[8,1,1536]{2,1,0:T(1,128)} %get-tuple-element.10.parts_ref), custom_call_target="tpu_custom_call" | custom-call | tf_op jit(solution)/shard_map/finish/pallas_call | solution.py:186
  470.2 1.1 slice_reduce_fusion
  471.3 0.6 reshape_squeeze.3
  471.9 1.3 reduce
  (1 shorter events, 0.0 us)
